TPU v7x, 256 devices: a whole 4x4x8 slice. The times are simulated.
256 devices in a mesh: fsdp: 32 (over z, y), ep: 8 (over x, core).
Axes of the slice: x: 4, y: 4, z: 8, core: 2. Of those that a mesh axis runs over, the one named last changes fastest.
Arguments:
- x_tok: bfloat16 [65536, 768], P(('fsdp', 'ep'))
- dy_tok: bfloat16 [65536, 768], P(('fsdp', 'ep'))
- expert_ids: int32 [65536, 2], P(('fsdp', 'ep'))
- route_w: float32 [65536, 2], P(('fsdp', 'ep'))
- w_gate: bfloat16 [8, 768, 2048], P('ep', 'fsdp')
- w_up: bfloat16 [8, 768, 2048], P('ep', 'fsdp')
- w_down: bfloat16 [8, 2048, 768], P('ep', None, 'fsdp')
Outputs:
- output 1: bfloat16 [65536, 768], P(('fsdp', 'ep'))
- output 2: float32 [65536, 2], P(('fsdp', 'ep'))
- output 3: float32 [8, 768, 2048], P('ep', 'fsdp')
- output 4: float32 [8, 768, 2048], P('ep', 'fsdp')
- output 5: float32 [8, 2048, 768], P('ep', None, 'fsdp')
All inputs are finite; a program needn't handle non-finite values.
Results may differ from a plain program's by a relative error of at most 0.00122.
Values are sent between devices in bfloat16 or wider.
A program may use at most 768 MiB of HBM per device.

v0:
```python
import jax
import jax.numpy as jnp
from jax import lax
from jax.sharding import PartitionSpec as P

CAP_FACTOR = 3


def capacity_of(tok_dev, top_k, experts):
    return max(8, ((CAP_FACTOR * tok_dev * top_k // experts + 7) // 8) * 8)


def route_slots(ids_dev, experts, capacity):
    n_pairs = ids_dev.shape[0]
    n_slots = experts * capacity
    onehot = (ids_dev[:, None] == jnp.arange(experts, dtype=jnp.int32)[None, :]).astype(jnp.int32)
    before = jnp.cumsum(onehot, axis=0) - onehot
    position = jnp.sum(before * onehot, axis=1)
    dest_slot = jnp.where(position < capacity, ids_dev * capacity + position, n_slots)
    held = jax.ops.segment_sum(jnp.arange(1, n_pairs + 1, dtype=jnp.int32), dest_slot, num_segments=n_slots + 1)[:n_slots]
    slot_src = jnp.where(held > 0, held - 1, n_pairs)
    return dest_slot, slot_src


def swiglu_grads(pre_gate, pre_up, grad_hidden):
    sigma = jax.nn.sigmoid(pre_gate)
    grad_gate = grad_hidden * pre_up * sigma * (1.0 + pre_gate * (1.0 - sigma))
    grad_up = grad_hidden * pre_gate * sigma
    return grad_gate.astype(jnp.bfloat16), grad_up.astype(jnp.bfloat16)


def expert_backward(x_rows, dy_rows, gate_rows, w_gate_full, w_up_full, w_down_full):
    pre_gate = jnp.einsum("secd,edf->secf", x_rows, w_gate_full, preferred_element_type=jnp.float32)
    pre_up = jnp.einsum("secd,edf->secf", x_rows, w_up_full, preferred_element_type=jnp.float32)
    hidden = (jax.nn.silu(pre_gate) * pre_up).astype(jnp.bfloat16)
    y_rows = jnp.einsum("secf,efd->secd", hidden, w_down_full, preferred_element_type=jnp.float32)
    dy_wide = dy_rows.astype(jnp.float32)
    scaled_dy = (gate_rows[..., None] * dy_wide).astype(jnp.bfloat16)
    dr_rows = jnp.sum(dy_wide * y_rows, axis=-1)
    grad_hidden = jnp.einsum("secd,efd->secf", scaled_dy, w_down_full, preferred_element_type=jnp.float32)
    grad_gate, grad_up = swiglu_grads(pre_gate, pre_up, grad_hidden)
    dx_rows = (jnp.einsum("secf,edf->secd", grad_gate, w_gate_full, preferred_element_type=jnp.float32)
               + jnp.einsum("secf,edf->secd", grad_up, w_up_full, preferred_element_type=jnp.float32)).astype(jnp.bfloat16)
    dw_gate = jnp.einsum("secd,secf->edf", x_rows, grad_gate, preferred_element_type=jnp.float32)
    dw_up = jnp.einsum("secd,secf->edf", x_rows, grad_up, preferred_element_type=jnp.float32)
    dw_down = jnp.einsum("secf,secd->efd", hidden, scaled_dy, preferred_element_type=jnp.float32)
    return dx_rows, dr_rows, dw_gate, dw_up, dw_down


def take_rows(rows, row_ids):
    return jnp.take(rows, row_ids, axis=0, mode="fill", fill_value=0)


def solution(mesh):
    n_ep = mesh.shape["ep"]
    tok_spec = P(("fsdp", "ep"), None)
    spec_in = P("ep", "fsdp", None)
    spec_out = P("ep", None, "fsdp")

    def per_device(x_tok, dy_tok, expert_ids, route_w, w_gate, w_up, w_down):
        tok_dev, top_k = expert_ids.shape
        exp_local = w_gate.shape[0]
        d_model = x_tok.shape[1]
        experts = exp_local * n_ep
        capacity = capacity_of(tok_dev, top_k, experts)
        dest_slot, slot_src = route_slots(expert_ids.reshape(-1), experts, capacity)
        tok_of_slot = slot_src // top_k
        x_send = take_rows(x_tok, tok_of_slot)
        dy_send = take_rows(dy_tok, tok_of_slot)
        gate_send = take_rows(route_w.reshape(-1), slot_src)
        x_recv = lax.all_to_all(x_send, "ep", 0, 0, tiled=True).reshape(n_ep, exp_local, capacity, d_model)
        dy_recv = lax.all_to_all(dy_send, "ep", 0, 0, tiled=True).reshape(n_ep, exp_local, capacity, d_model)
        gate_recv = lax.all_to_all(gate_send, "ep", 0, 0, tiled=True).reshape(n_ep, exp_local, capacity)
        w_gate_full = lax.all_gather(w_gate, "fsdp", axis=1, tiled=True)
        w_up_full = lax.all_gather(w_up, "fsdp", axis=1, tiled=True)
        w_down_full = lax.all_gather(w_down, "fsdp", axis=2, tiled=True)
        dx_rows, dr_rows, dw_gate, dw_up, dw_down = expert_backward(
            x_recv, dy_recv, gate_recv, w_gate_full, w_up_full, w_down_full)
        dx_back = lax.all_to_all(dx_rows.reshape(n_ep * exp_local * capacity, d_model), "ep", 0, 0, tiled=True)
        dr_back = lax.all_to_all(dr_rows.reshape(-1), "ep", 0, 0, tiled=True)
        dx_pairs = take_rows(dx_back, dest_slot).reshape(tok_dev, top_k, d_model)
        grad_x = jnp.sum(dx_pairs.astype(jnp.float32), axis=1).astype(jnp.bfloat16)
        route_grad = take_rows(dr_back, dest_slot).reshape(tok_dev, top_k)
        grad_w_gate = lax.psum_scatter(dw_gate, "fsdp", scatter_dimension=1, tiled=True)
        grad_w_up = lax.psum_scatter(dw_up, "fsdp", scatter_dimension=1, tiled=True)
        grad_w_down = lax.psum_scatter(dw_down, "fsdp", scatter_dimension=2, tiled=True)
        return grad_x, route_grad, grad_w_gate, grad_w_up, grad_w_down

    return jax.shard_map(
        per_device, mesh=mesh,
        in_specs=(tok_spec, tok_spec, tok_spec, tok_spec, spec_in, spec_in, spec_out),
        out_specs=(tok_spec, tok_spec, spec_in, spec_in, spec_out),
        check_vma=False)
```

profile of v0, /device:TPU:2, one launch (start us, length us, event | category | flops | bytes accessed | tf_op | source)
XLA Modules:
  0.0 944.1 jit_solution(1557451527711360090)
XLA Ops:
  7.2 0.7 all-gather.8.cloned.1.call-update
  8.0 0.7 all-gather.4.cloned.1.call-update
  8.7 0.8 copy.22
  9.5 0.1 eq.29
  9.8 1.1 reduce-window.6
  10.9 0.2 slice_reduce_fusion
  11.3 0.8 copy.25
  12.4 3.5 scatter_custom_fusion
  16.0 9.5 %gather_fusion = f32[1536]{0:T(1024)S(1)} fusion(f32[512]{0:T(512)S(1)} %reshape.234, s32[2048]{0:T(1024)S(1)} %pad_clamp_fusion.1), kind=kCustom, calls=%fused_computation.2 | custom fusion | bytes 18432 | tf_op jit(solution)/shard_map/jit(_take)/gather | solution.py:51
  25.6 0.6 and_select_fusion
  26.3 5.4 all-to-all-start
  31.7 0.7 all-gather.6.cloned.1.call-update
  32.4 5.0 gather_fusion.3
  37.4 5.7 gather_fusion.4
  43.1 4.0 broadcast_select_fusion
  47.1 33.3 %all_to_all.45 = bf16[8,192,768]{2,1,0:T(8,128)(2,1)} all-to-all(bf16[8,192,768]{2,1,0:T(8,128)(2,1)} %bitcast.148), channel_id=1, replica_groups=mesh['fsdp'=32,'ep'=8] {'ep'}, dimensions={0} | all-to-all | bytes 4718592 | tf_op jit(solution)/shard_map/all_to_all | solution.py:71
  80.3 5.0 all-to-all-start.1
  85.3 7.7 all-gather.8.cloned.1.call-done
  93.0 10.1 %fusion.38 = f32[8,192,2048]{2,1,0:T(8,128)} fusion(bf16[8,192,768]{2,1,0:T(8,128)(2,1)} %all_to_all.45, bf16[1,768,2048]{2,1,0:T(8,128)(2,1)} %all-gather.8.cloned.1.call-done), kind=kOutput, calls=%fused_computation.47 | convolution fusion | flops 4831838208 | bytes 18087936 | tf_op jit(solution)/shard_map/secd,edf->secf/dot_general | solution.py:33
  103.1 10.8 %all-to-all-done.1 = bf16[8,192,768]{2,1,0:T(8,128)(2,1)S(1)} async-done(((bf16[8,192,768]{2,1,0:T(8,128)(2,1)}), bf16[8,192,768]{2,1,0:T(8,128)(2,1)S(1)}, u32[]{:S(2)}, u32[]{:S(2)}) %all-to-all-start.1) | async-done | bytes 2359328 | tf_op jit(solution)/shard_map/all_to_all | solution.py:72
  113.9 58.0 %all-gather.4.cloned.1.call-done = bf16[1,2048,768]{1,2,0:T(8,128)(2,1)} async-done(((bf16[1,2048,24]{1,2,0:T(8,128)(2,1)}), bf16[1,2048,768]{1,2,0:T(8,128)(2,1)}) %all-gather.4.cloned.1.call-update) | async-done | bytes 3145744 | tf_op jit(solution)/shard_map/all_gather | solution.py:76
  171.9 10.0 %fusion.35 = f32[8,192,2048]{2,1,0:T(8,128)} fusion(bf16[1,2048,768]{1,2,0:T(8,128)(2,1)} %all-gather.4.cloned.1.call-done, bf16[8,192,768]{2,1,0:T(8,128)(2,1)S(1)} %all-to-all-done.1, f32[8,192]{1,0:T(8,128)S(1)} %bitcast.150), kind=kOutput, calls=%fused_computation.44 | convolution fusion | flops 4835377152 | bytes 18094080 | tf_op jit(solution)/shard_map/secd,efd->secf/dot_general | solution.py:40
  181.9 68.7 %all-gather.6.cloned.1.call-done = bf16[1,768,2048]{2,1,0:T(8,128)(2,1)} async-done(((bf16[1,24,2048]{2,1,0:T(8,128)(2,1)}), bf16[1,768,2048]{2,1,0:T(8,128)(2,1)}) %all-gather.6.cloned.1.call-update) | async-done | bytes 3145744 | tf_op jit(solution)/shard_map/all_gather | solution.py:75
  250.6 21.3 %fusion.3 = (bf16[8,1,192,2048]{3,2,0,1:T(8,128)(2,1)}, bf16[8,1,192,2048]{3,2,0,1:T(8,128)(2,1)}, bf16[8,1,192,2048]{3,2,0,1:T(8,128)(2,1)}) fusion(f32[8,192,2048]{2,1,0:T(8,128)} %fusion.38, f32[8,192,2048]{2,1,0:T(8,128)} %fusion.35, bf16[8,192,768]{2,1,0:T(8,128)(2,1)} %all_to_all.45, bf16[1,768,2048]{2,1,0:T(8,128)(2,1)} %all-gather.6.cloned.1.call-done), kind=kOutput, calls=%fused_computation.11 | convolution fusion | flops 4882169856 | bytes 49545216 | tf_op jit(solution)/shard_map/secd,edf->secf/dot_general | solution.py:34
  271.9 10.7 %fusion.31 = f32[1,2048,768]{2,1,0:T(8,128)} fusion(bf16[8,1,192,2048]{3,2,0,1:T(8,128)(2,1)} %get-tuple-element.27, bf16[8,192,768]{2,1,0:T(8,128)(2,1)S(1)} %all-to-all-done.1, f32[8,192]{1,0:T(8,128)S(1)} %bitcast.151), kind=kOutput, calls=%fused_computation.42 | convolution fusion | flops 4835377152 | bytes 14948352 | tf_op jit(solution)/shard_map/secf,secd->efd/dot_general | solution.py:46
  282.6 15.9 %copy.27 = f32[1,2048,768]{1,0,2:T(1,128)} copy(f32[1,2048,768]{2,1,0:T(8,128)} %fusion.31) | data formatting | bytes 12582912 | tf_op jit(solution)/shard_map/secf,secd->efd/dot_general | solution.py:46
  298.6 0.3 reduce-scatter.5.cloned.1.call-start
  298.8 9.7 %fusion.28 = f32[1,768,2048]{2,1,0:T(8,128)} fusion(bf16[8,192,768]{2,1,0:T(8,128)(2,1)} %all_to_all.45, bf16[8,1,192,2048]{3,2,0,1:T(8,128)(2,1)} %get-tuple-element.29), kind=kOutput, calls=%fused_computation.41 | convolution fusion | flops 4831838208 | bytes 14942208 | tf_op jit(solution)/shard_map/secd,secf->edf/dot_general | solution.py:45
  308.6 9.6 %fusion.25 = f32[1,768,2048]{2,1,0:T(8,128)} fusion(bf16[8,192,768]{2,1,0:T(8,128)(2,1)} %all_to_all.45, bf16[8,1,192,2048]{3,2,0,1:T(8,128)(2,1)} %get-tuple-element.28), kind=kOutput, calls=%fused_computation.40 | convolution fusion | flops 4831838208 | bytes 14942208 | tf_op jit(solution)/shard_map/secd,secf->edf/dot_general | solution.py:44
  318.3 8.3 fusion.24
  326.6 0.6 all_to_all.37
  327.3 4.8 all-to-all-start.4
  332.1 8.3 fusion.16
  340.4 9.5 %add_convert_fusion = bf16[8,192,768]{2,1,0:T(8,128)(2,1)} fusion(f32[8,192,768]{2,1,0:T(8,128)S(1)} %fusion.16, bf16[1,768,2048]{2,1,0:T(8,128)(2,1)S(1)} %copy-done.3, bf16[8,1,192,2048]{3,2,0,1:T(8,128)(2,1)} %get-tuple-element.28), kind=kOutput, calls=%fused_computation.39 | convolution fusion | flops 4834197504 | bytes 16515072 | tf_op jit(solution)/shard_map/secf,edf->secd/dot_general | solution.py:42
  349.9 5.0 all-to-all-start.3
  355.0 0.6 dynamic-slice
  356.4 3.1 gather_fusion.2
  359.7 0.7 broadcast_select_fusion.3
  360.3 0.7 copy.28
  361.0 22.4 %all-to-all-done.3 = bf16[8,192,768]{2,1,0:T(8,128)(2,1)S(1)} async-done(((bf16[8,192,768]{2,1,0:T(8,128)(2,1)}), bf16[8,192,768]{2,1,0:T(8,128)(2,1)S(1)}, u32[]{:S(2)}, u32[]{:S(2)}) %all-to-all-start.3) | async-done | bytes 2359328 | tf_op jit(solution)/shard_map/all_to_all | solution.py:79
  383.4 2.0 gather_fusion.1
  385.4 0.3 gather.24
  385.7 3.8 fusion.53
  389.5 89.8 %all-reduce.3.cloned.1.call-done = f32[1,2048,768]{1,0,2:T(1,128)} async-done(((f32[1,2048,768]{1,0,2:T(1,128)}), f32[1,2048,768]{1,0,2:T(1,128)}) %all-reduce.3.cloned.1.call-update) | async-done | bytes 6291472
  479.3 0.9 constant_dynamic-slice_fusion
  480.2 0.7 copy.29
  481.0 227.5 %reduce-scatter.5.cloned.1.call-done = f32[1,24,2048]{2,1,0:T(8,128)} async-done(((f32[1,768,2048]{2,1,0:T(8,128)}), f32[1,24,2048]{2,1,0:T(8,128)}) %reduce-scatter.5.cloned.1.call-update) | async-done | bytes 196624 | tf_op jit(solution)/shard_map/reduce_scatter | solution.py:85
  708.4 228.9 %reduce-scatter.3.cloned.1.call-done = f32[1,24,2048]{2,1,0:T(8,128)} async-done(((f32[1,768,2048]{2,1,0:T(8,128)}), f32[1,24,2048]{2,1,0:T(8,128)}) %reduce-scatter.3.cloned.1.call-update) | async-done | bytes 196624 | tf_op jit(solution)/shard_map/reduce_scatter | solution.py:84
  (42 shorter events, 1.4 us)
Async XLA Ops:
  7.2 25.2 %copy-start = (bf16[256,768]{1,0:T(8,128)(2,1)S(1)}, bf16[256,768]{1,0:T(8,128)(2,1)}, u32[]{:S(2)}) copy-start(bf16[256,768]{1,0:T(8,128)(2,1)} %param.10) | copy-start | bytes 1179652
  7.2 85.8 %all-gather.8.cloned.1.call-start = ((), (), s32[]{:S(2)}) async-start(), calls=%async_computation.9 | async-start | bytes 3244032 | tf_op jit(solution)/shard_map/all_gather | solution.py:74
  7.9 164.0 %all-gather.4.cloned.1.call-start = ((), (), s32[]{:S(2)}) async-start(), calls=%async_computation.7 | async-start | bytes 3244032 | tf_op jit(solution)/shard_map/all_gather | solution.py:76
  26.3 20.8 %all-to-all-start = ((f32[8,192,1]{1,2,0:T(1,128)}), f32[8,192,1]{1,2,0:T(1,128)S(1)}, u32[]{:S(2)}, u32[]{:S(2)}) async-start(f32[8,192,1]{1,2,0:T(1,128)} %and_select_fusion), calls=%async_computation | async-start | bytes 16384 | tf_op jit(solution)/shard_map/all_to_all | solution.py:73
  31.7 218.9 %all-gather.6.cloned.1.call-start = ((), (), s32[]{:S(2)}) async-start(), calls=%async_computation.8 | async-start | bytes 3244032 | tf_op jit(solution)/shard_map/all_gather | solution.py:75
  32.4 5.0 copy-start.2
  80.3 33.6 %all-to-all-start.1 = ((bf16[8,192,768]{2,1,0:T(8,128)(2,1)}), bf16[8,192,768]{2,1,0:T(8,128)(2,1)S(1)}, u32[]{:S(2)}, u32[]{:S(2)}) async-start(bf16[8,192,768]{2,1,0:T(8,128)(2,1)} %bitcast.4), calls=%async_computation.1 | async-start | bytes 4718592 | tf_op jit(solution)/shard_map/all_to_all | solution.py:72
  85.3 394.0 %all-reduce.3.cloned.1.call-start = ((), (), s32[]{:S(2)}) async-start(), calls=%async_computation.12 | async-start | bytes 12582912
  298.6 409.9 %reduce-scatter.5.cloned.1.call-start = ((), (), s32[]{:S(2)}) async-start(), calls=%async_computation.11 | async-start | bytes 6488064 | tf_op jit(solution)/shard_map/reduce_scatter | solution.py:85
  308.6 628.7 %reduce-scatter.3.cloned.1.call-start = ((), (), s32[]{:S(2)}) async-start(), calls=%async_computation.10 | async-start | bytes 6488064 | tf_op jit(solution)/shard_map/reduce_scatter | solution.py:84
  327.3 22.7 %all-to-all-start.4 = ((f32[8,192,1]{1,2,0:T(1,128)}), f32[8,192,1]{1,2,0:T(1,128)S(1)}, u32[]{:S(2)}, u32[]{:S(2)}) async-start(f32[8,192,1]{1,2,0:T(1,128)} %all_to_all.37), calls=%async_computation.4 | async-start | bytes 16384 | tf_op jit(solution)/shard_map/all_to_all | solution.py:80
  332.1 8.3 copy-start.3
  349.9 5.1 copy-start.4
  349.9 33.5 %all-to-all-start.3 = ((bf16[8,192,768]{2,1,0:T(8,128)(2,1)}), bf16[8,192,768]{2,1,0:T(8,128)(2,1)S(1)}, u32[]{:S(2)}, u32[]{:S(2)}) async-start(bf16[8,192,768]{2,1,0:T(8,128)(2,1)} %add_convert_fusion), calls=%async_computation.3 | async-start | bytes 4718592 | tf_op jit(solution)/shard_map/all_to_all | solution.py:79
  383.4 553.9 %copy-start.1 = (bf16[256,768]{1,0:T(8,128)(2,1)S(1)}, bf16[256,768]{1,0:T(8,128)(2,1)}, u32[]{:S(2)}) copy-start(bf16[256,768]{1,0:T(8,128)(2,1)} %param.10) | copy-start | bytes 1179652
Sparse Core Ops, SparseCore 0:
  10.6 82.4 all-gather.7
  95.6 76.2 all-gather.3
  174.5 76.0 all-gather.5
  298.7 180.5 all-reduce.2
  483.7 224.6 reduce-scatter.4
  712.8 224.4 reduce-scatter.2
where the time goes:
time: 945 us; the launch traced here: 944 us
  waiting for transfers between devices  716 us (76%)
  matrix products  97.6 us (10%)
  local copies, waits for them, and re-layouts  48 us (5%)
  blocking collectives  33.3 us (4%)
  starting transfers between devices  20.5 us (2%)
  between operations  15 us (2%)
  other arithmetic  14 us (1%)
    reduce_scatter x1, waiting for transfers between devices, per_device(): lax.psum_scatter(dw_gate, 'fsdp', scatter_dimension=1, tiled=True)  229 us
    reduce_scatter x1, waiting for transfers between devices, per_device(): grad_w_up = lax.psum_scatter(dw_up, 'fsdp', scatter_dimension=1, tiled=True)  227 us
    unnamed x7, waiting for transfers between devices  91.9 us
    all_gather x1, waiting for transfers between devices, per_device(): w_up_full = lax.all_gather(w_up, 'fsdp', axis=1, tiled=True)  68.7 us
    all_gather x1, waiting for transfers between devices, per_device(): w_down_full = lax.all_gather(w_down, 'fsdp', axis=2, tiled=True)  58 us
    all_to_all x1, blocking collectives, per_device(): lax.all_to_all(x_send, 'ep', 0, 0, tiled=True)  33.3 us
    gather x8, local copies, waits for them, and re-layouts, take_rows(): return jnp.take(rows, row_ids, axis=0, mode='fill', fill_value=0)  25.8 us
    all_to_all x1, waiting for transfers between devices, per_device(): lax.all_to_all(dx_rows.reshape(n_ep * exp_local * capacity, d_model), 'ep...  22.4 us
  transfers between devices with their start and end apart: 10, of which 8 were waited for; matrix products, arithmetic and copies ran while one was open for 12% of the time, Pallas kernels for 0%

commit v1 on v0

v1 whole, which is shorter than its diff:
```python
import jax
import jax.numpy as jnp
from jax import lax
from jax.experimental import pallas as pl
from jax.experimental.pallas import tpu as pltpu
from jax.sharding import PartitionSpec as P

CAP_FACTOR = 3
MESH = pl.DeviceIdType.MESH
NZ, NY, NX = 8, 4, 4
RING = NZ * NY
PEERS = 8


def capacity_of(tok_dev, top_k, experts):
    return max(8, ((CAP_FACTOR * tok_dev * top_k // experts + 7) // 8) * 8)


def signal_all(targets):
    barrier = pltpu.get_barrier_semaphore()
    for t in targets:
        pl.semaphore_signal(barrier, inc=1, device_id=t, device_id_type=MESH)
    pl.semaphore_wait(barrier, len(targets))


CHUNK = 256
ROWS = 512
SUB = 256
HOPS = 6
SERVE = (1, 3)
SETS = 4


def dot(a, b, ca, cb):
    return lax.dot_general(a, b, (((ca,), (cb,)), ((), ())), preferred_element_type=jnp.float32)


def moe_kernel(x_hbm, dy_hbm, ids_ref, r_ref, w1_ref, w3_ref, w2_ref, gx_out, rw_out, g1_out, g3_out, g2_out, x_all, dy_all,
               meta_ref, meta_all, dx_in, dr_in, tok, wbuf, dw, az_half, az, ay_part, ay, by_half, by, bz_part, bz,
               xs, dys, gs, xt, gt, hid, dx_acc, dr_acc, dr_send,
               tok_sem, loc_sem, tsend, trecv, wsend, wrecv, xsend, xrecv, gsend, grecv, free_sem):
    f32, bf16 = jnp.float32, jnp.bfloat16
    i, p = lax.axis_index("fsdp"), lax.axis_index("ep")
    z, y = lax.div(i, NY), lax.rem(i, NY)
    chip, core = lax.div(p, 2), lax.rem(p, 2)
    right, left, across = [lax.rem(chip + n, NX) for n in (1, NX - 1, 2)]
    xr, xl, xo = [n * 2 + core for n in (right, left, across)]
    partner, xpr, xpl, xpo = [n * 2 + 1 - core for n in (chip, right, left, across)]
    step_of = (1, -1)

    def zt(d, j):
        return lax.rem(z + step_of[d] * j + NZ, NZ)

    def yt(d, j):
        return lax.rem(y + step_of[d] * j + NY, NY)

    fz = [zt(d, 1) * NY + y for d in (0, 1)]
    fy = [z * NY + yt(d, 1) for d in (0, 1)]
    peer = [lax.rem(p + r, PEERS) for r in range(1, PEERS)]
    chunks = dw.shape[0]
    tiles = xs.shape[0] // ROWS
    cap = xs.shape[0] // PEERS
    half = CHUNK // 2
    ca, cb = pl.ds(0, half), pl.ds(half, half)

    tokens = ids_ref.shape[1]
    expert = lax.broadcasted_iota(jnp.int32, (PEERS, tokens), 0)
    hits = [expert == ids_ref[j:j + 1, :] for j in (0, 1)]
    used = jnp.logical_or(hits[0], hits[1])
    earlier = (lax.broadcasted_iota(jnp.int32, (tokens, tokens), 0)
               < lax.broadcasted_iota(jnp.int32, (tokens, tokens), 1))
    before = dot(jnp.where(used, 1.0, 0.0).astype(bf16), jnp.where(earlier, 1.0, 0.0).astype(bf16), 1, 0)
    meta_ref[0:PEERS, :] = jnp.where(used, before, float(cap))
    meta_ref[PEERS:2 * PEERS, :] = sum(jnp.where(hits[j], r_ref[j:j + 1, :], 0.0) for j in (0, 1))
    meta_all[p] = meta_ref[...]

    signal_all([{"fsdp": t} for t in fz + fy] + [{"ep": e} for e in peer])
    part = (pl.ds(0, 16), pl.ds(16, 8))

    def whop(c, h, v, d):
        cols = (ca, cb)[v]
        if h == 0:
            return wbuf.at[c, :, z, y, :, cols], (fy, fz)[v][d]
        if v == 0:
            if h == 1:
                return wbuf.at[c, :, z, yt(d, -1), part[d], cols], fy[d]
            if h < 5:
                return wbuf.at[c, :, zt(d, 2 - h), :, :, cols], fz[d]
            return wbuf.at[c, :, zt(d, -3), pl.ds(2 * d, 2), :, cols], fz[d]
        if h < 3:
            return wbuf.at[c, :, zt(d, -h), y, :, cols], fz[d]
        if h == 3:
            return wbuf.at[c, :, zt(d, -3), y, part[d], cols], fz[d]
        if h == 4:
            return wbuf.at[c, :, :, y, :, cols], fy[d]
        return wbuf.at[c, :, pl.ds(4 * d, 4), yt(d, -1), :, cols], fy[d]

    def wcopy(c, h, v, d):
        block, to = whop(c, h, v, d)
        return pltpu.make_async_remote_copy(
            src_ref=block, dst_ref=block, send_sem=wsend.at[c, v, d], recv_sem=wrecv.at[c, h, v, d],
            device_id={"fsdp": to}, device_id_type=MESH)

    def gather_round(a):
        def one(c, carry):
            for h in range(HOPS + 1):
                @pl.when(a - c == h)
                def _(h=h):
                    for v in (0, 1):
                        together = h == (2, 4)[v]
                        for d in (0, 1):
                            if h:
                                wcopy(c, h - 1, v, d).wait_recv()
                                wcopy(c, h - 1, v, d).wait_send()
                            if h < HOPS and not together:
                                wcopy(c, h, v, d).start()
                        if together:
                            for d in (0, 1):
                                wcopy(c, h, v, d).start()
            return carry
        lax.fori_loop(lax.max(a - HOPS, 0), lax.min(a + 1, chunks), one, 0)

    def tcopy(n, which, block, to, own_block=False):
        src, dst = ((x_hbm, x_all), (dy_hbm, dy_all), (meta_ref, meta_all))[which]
        return pltpu.make_async_remote_copy(
            src_ref=src if own_block else dst.at[block], dst_ref=dst.at[block],
            send_sem=tsend.at[n], recv_sem=trecv.at[n],
            device_id={"ep": to}, device_id_type=MESH)

    def arrived(r, block):
        for w in (2, 0, 1):
            tcopy(3 * r + w, w, block, partner).wait_recv()

    def fetch(slot, block=None):
        for w, (own, ref) in enumerate(((x_hbm, x_all), (dy_hbm, dy_all))):
            yield pltpu.make_async_copy(own if block is None else ref.at[block], tok.at[slot, w], tok_sem.at[slot, w])

    def picked(place):
        return lax.broadcasted_iota(jnp.int32, (cap, tokens), 0).astype(f32) == place

    def build(slot, copies, meta, src):
        for c in copies:
            c.wait()
        place, weight = meta[pl.ds(p, 1), :], meta[pl.ds(PEERS + p, 1), :]
        pick = picked(place)
        rows = pl.ds(pl.multiple_of(src * cap, cap), cap)
        onehot = jnp.where(pick, 1.0, 0.0).astype(bf16)
        xs[rows, :] = dot(onehot, tok[slot, 0], 1, 0).astype(bf16)
        dy = dot(onehot, tok[slot, 1], 1, 0).astype(bf16)
        dys[rows, :] = dy
        gate = jnp.sum(jnp.where(pick, weight, 0.0), axis=1, keepdims=True)
        gs[rows, :] = (gate * dy.astype(f32)).astype(bf16)

    def build_pair(k, first, second):
        loads = [list(fetch(slot, None if src is None else src)) for slot, src in enumerate((first, second))]
        for cs in loads:
            for c in cs:
                c.start()
        for slot, src in enumerate((first, second)):
            build(slot, loads[slot], meta_ref if src is None else meta_all.at[src], p if src is None else src)
        both = pl.ds(pl.multiple_of(k * 2 * cap, 2 * cap), 2 * cap)
        xt[:, both] = jnp.transpose(xs[both, :])
        gt[:, both] = jnp.transpose(gs[both, :])

    def hop_a(c, h, d):
        if h == 0:
            return dw.at[c, :, zt(d, 4), pl.ds(2 * d, 2), :, ca], az_half.at[lax.rem(c, SETS), d], fz[d]
        if h < 4:
            return dw.at[c, :, zt(d, 4 - h), :, :, ca], az.at[lax.rem(c, SETS), d, h - 1], fz[d]
        if h == 4:
            return dw.at[c, :, z, yt(d, 2), part[d], ca], ay_part.at[lax.rem(c, SETS), d, :, pl.ds(0, part[d].size)], fy[d]
        return dw.at[c, :, z, yt(d, 1), :, ca], ay.at[lax.rem(c, SETS), d], fy[d]

    def land_a(c, h, d):
        if h == 0:
            return dw.at[c, :, zt(d, 3), pl.ds(2 * d, 2), :, ca]
        if h < 4:
            return dw.at[c, :, zt(d, 3 - h), :, :, ca]
        if h == 4:
            return dw.at[c, :, z, yt(d, 1), part[d], ca]
        return dw.at[c, :, z, y, :, ca]

    def hop_b(c, h, d):
        if h == 0:
            return dw.at[c, :, pl.ds(4 * d, 4), yt(d, 2), :, cb], by_half.at[lax.rem(c, SETS), d], fy[d]
        if h == 1:
            return dw.at[c, :, :, yt(d, 1), :, cb], by.at[lax.rem(c, SETS), d], fy[d]
        if h == 2:
            return dw.at[c, :, zt(d, 4), y, part[d], cb], bz_part.at[lax.rem(c, SETS), d, :, pl.ds(0, part[d].size)], fz[d]
        return dw.at[c, :, zt(d, 6 - h), y, :, cb], bz.at[lax.rem(c, SETS), d, h - 3], fz[d]

    def land_b(c, h, d):
        if h == 0:
            return dw.at[c, :, pl.ds(4 * d, 4), yt(d, 1), :, cb]
        if h == 1:
            return dw.at[c, :, :, y, :, cb]
        if h == 2:
            return dw.at[c, :, zt(d, 3), y, part[d], cb]
        return dw.at[c, :, zt(d, 5 - h), y, :, cb]

    rounds = len(SERVE)
    plans = ((hop_a, land_a), (hop_b, land_b))
    last_of_phase = ((3, 5), (1, 5))

    def gcopy(c, h, v, d):
        src, dst, to = plans[v][0](c, h, d)
        return pltpu.make_async_remote_copy(
            src_ref=src, dst_ref=dst, send_sem=gsend.at[c, v, d], recv_sem=grecv.at[c, h, v, d],
            device_id={"fsdp": to}, device_id_type=MESH)

    def arrive(c, h, v, d):
        gcopy(c, h, v, d).wait_recv()
        gcopy(c, h, v, d).wait_send()
        into, slot = plans[v][1](c, h, d), plans[v][0](c, h, d)[1]
        into[...] = into[...] + slot[...]

    def serve(q):
        lo = lax.max(lax.div(q - HOPS + rounds - 1 + rounds * chunks, rounds) - chunks - 1, 0)
        hi = lax.min(lax.div(q, rounds), chunks)

        def one(c, carry):
            s = q - (c + 1) * rounds
            for h in range(HOPS + 1):
                @pl.when(s == h)
                def _(h=h):
                    if h == 0:
                        @pl.when(c >= SETS)
                        def _():
                            pl.semaphore_wait(free_sem.at[lax.max(c - SETS, 0)], 4)
                    for v in (0, 1):
                        together = h - 1 in last_of_phase[v]
                        if together:
                            for d in (0, 1):
                                arrive(c, h - 1, v, d)
                        for d in (0, 1):
                            if h and not together:
                                arrive(c, h - 1, v, d)
                            if h < HOPS:
                                gcopy(c, h, v, d).start()
                    if h == HOPS:
                        out = pl.ds(pl.multiple_of(c * CHUNK, CHUNK), CHUNK)
                        for n, g in enumerate((g1_out, g3_out, g2_out)):
                            g[:, out] = dw[c, n, z, y]

                        @pl.when(c + SETS < chunks)
                        def _():
                            for t in fz + fy:
                                pl.semaphore_signal(free_sem.at[lax.min(c, chunks - SETS - 1)], inc=1,
                                                    device_id={"fsdp": t}, device_id_type=MESH)
            return carry
        lax.fori_loop(lo, hi, one, 0)

    def forward(c, r):
        w = [wbuf[c, n].reshape(xs.shape[1], CHUNK) for n in range(3)]
        for m in range(r * ROWS, (r + 1) * ROWS, SUB):
            rows = pl.ds(m, SUB)
            h1, h3 = dot(xs[rows, :], w[0], 1, 0), dot(xs[rows, :], w[1], 1, 0)
            da, u = dot(gs[rows, :], w[2], 1, 0), dot(dys[rows, :], w[2], 1, 0)
            s = jax.nn.sigmoid(h1)
            a = (h1 * s * h3).astype(bf16)
            hid[0, rows, :] = (da * h3 * s * (1.0 + h1 * (1.0 - s))).astype(bf16)
            hid[1, rows, :] = (da * h1 * s).astype(bf16)
            hid[2, rows, :] = a
            au = a.astype(f32) * u
            dr_acc[rows, :] += au[:, :128] + au[:, 128:]

    def back(c, r):
        w = [wbuf[c, n].reshape(xs.shape[1], CHUNK) for n in range(3)]
        for m in range(r * ROWS, (r + 1) * ROWS, SUB):
            rows = pl.ds(m, SUB)
            dx_acc[rows, :] += dot(hid[0, rows, :], w[0], 1, 1) + dot(hid[1, rows, :], w[1], 1, 1)

    def weight_grads(c):
        for n, t in enumerate((xt, xt, gt)):
            dw[c, n] = dot(t[...], hid[n], 1, 0).reshape(dw.shape[2:])

    first_sends = [tcopy(3 * r + w, w, p, to, True) for r, to in ((0, xr), (1, xl), (2, partner)) for w in (2, 0, 1)]
    for c in first_sends:
        c.start()

    def own_piece(c, carry):
        for n, w in enumerate((w1_ref, w3_ref, w2_ref)):
            wbuf[c, n, z, y] = w[:, pl.ds(pl.multiple_of(c * CHUNK, CHUNK), CHUNK)]
        return carry
    lax.fori_loop(0, chunks, own_piece, 0)
    dr_acc[...] = jnp.zeros_like(dr_acc)
    dx_acc[...] = jnp.zeros_like(dx_acc)

    second = [tcopy(n, w, src, to) for n, w, src, to in
              ((18 + 2, 2, xl, xr), (18 + 1, 1, xl, xr), (18 + 0, 0, xr, xl))]
    forward_lr = [tcopy(3 * r + w, w, src, partner) for r, src in ((3, xl), (4, xr)) for w in (2, 0, 1)]
    forward_o = [tcopy(15 + w, w, xo, partner) for w in (2, 0, 1)]

    def back_block(which, q):
        return xs.at[pl.ds(pl.multiple_of(q * cap, cap), cap)] if which == 0 else dr_send.at[q]

    def xcopy(r, which, dst_peer, slot):
        return pltpu.make_async_remote_copy(
            src_ref=back_block(which, dst_peer), dst_ref=(dx_in, dr_in)[which].at[slot],
            send_sem=xsend.at[r, which], recv_sem=xrecv.at[r, which],
            device_id={"ep": dst_peer}, device_id_type=MESH)

    own = [pltpu.make_async_copy(back_block(n, p), d.at[p], loc_sem.at[n]) for n, d in enumerate((dx_in, dr_in))]
    sent = [[xcopy(r, w, peer[r], p) for r in range(PEERS - 1)] for w in (0, 1)]

    def tokens_1():
        arrived(2, partner)
        build_pair(chip, None, partner)

    def tokens_3():
        arrived(0, xl)
        arrived(1, xr)
        for c in second + forward_lr:
            c.start()

    def tokens_4():
        arrived(3, xpl)
        build_pair(left, xl, xpl)

    def tokens_5():
        arrived(4, xpr)
        build_pair(right, xr, xpr)
        arrived(6, xo)
        for c in forward_o:
            c.start()

    def tokens_6():
        arrived(5, xpo)
        build_pair(across, xo, xpo)

    def send_back():
        xs[...] = dx_acc[...].astype(bf16)
        for c in own[:1] + sent[0]:
            c.start()
        for e in range(PEERS):
            total = jnp.sum(dr_acc[e * cap:(e + 1) * cap, :], axis=1, keepdims=True)
            here = picked(meta_all[e, pl.ds(p, 1), :])
            dr_send[e, 0:1, :] = jnp.sum(jnp.where(here, total, 0.0), axis=0, keepdims=True)
        for c in own[1:] + sent[1]:
            c.start()

    def combine():
        for r in range(PEERS - 1):
            for w in (0, 1):
                xcopy(r, w, peer[r], lax.rem(p + PEERS - 1 - r, PEERS)).wait_recv()
        for c in own:
            c.wait()
        gx = jnp.zeros(gx_out.shape, f32)
        rw = [jnp.zeros((1, tokens), f32) for _ in (0, 1)]
        for e in range(PEERS):
            here = jnp.where(picked(meta_ref[e:e + 1, :]), 1.0, 0.0).astype(bf16)
            gx = gx + dot(here, dx_in[e], 0, 0)
            rw = [rw[j] + jnp.where(ids_ref[j:j + 1, :] == e, dr_in[e, 0:1, :], 0.0) for j in (0, 1)]
        gx_out[...] = gx.astype(bf16)
        for j in (0, 1):
            rw_out[j:j + 1, :] = rw[j]

    def compute(c, r):
        if r < tiles:
            forward(c, r)
        else:
            weight_grads(c)
        if r:
            back(c, r - 1)

    lead = HOPS + 1
    steps = lead + rounds * chunks

    def step(t, carry):
        n = t - lead
        c, r = lax.div(lax.max(n, 0), rounds), lax.rem(lax.max(n, 0), rounds)
        for j in range(rounds):
            @pl.when(jnp.logical_and(jnp.logical_and(n >= 0, t < steps), r == j))
            def _(j=j):
                for u in range(0 if j == 0 else SERVE[j - 1] + 1, SERVE[j] + 1):
                    compute(c, u)

        @pl.when(r == 0)
        def _():
            gather_round(lax.min(t, lead) + c)
        for at, event in ((1, tokens_1), (3, tokens_3), (4, tokens_4), (5, tokens_5), (6, tokens_6),
                          (steps, send_back), (steps + HOPS - 1, combine)):
            pl.when(t == at)(event)

        @pl.when(n >= 0)
        def _():
            serve(n + 1)
        return carry
    lax.fori_loop(0, steps + HOPS, step, 0)

    for c in first_sends + second + forward_lr + forward_o + sent[0] + sent[1]:
        c.wait_send()


def moe_step(x_tok, dy_tok, ids, route, w1, w3, w2t, capacity):
    tok_dev, d_model = x_tok.shape
    width = w1.shape[1]
    n_rows = PEERS * capacity
    block, chunks, half = d_model // RING, width // CHUNK, CHUNK // 2
    f32, bf16 = jnp.float32, jnp.bfloat16
    vmem = pl.BlockSpec(memory_space=pltpu.VMEM)
    hbm = pl.BlockSpec(memory_space=pl.ANY)
    dma = pltpu.SemaphoreType.DMA
    landing = jax.ShapeDtypeStruct((PEERS, tok_dev, d_model), bf16)
    grad = jax.ShapeDtypeStruct((block, width), f32)
    meta = jax.ShapeDtypeStruct((2 * PEERS, tok_dev), f32)
    return pl.pallas_call(
        moe_kernel,
        out_shape=(jax.ShapeDtypeStruct((tok_dev, d_model), bf16), jax.ShapeDtypeStruct(route.shape, f32),
                   grad, grad, grad, landing, landing),
        in_specs=[hbm, hbm] + [vmem] * 5,
        out_specs=[vmem] * 5 + [hbm, hbm],
        scratch_shapes=[
            pltpu.VMEM(meta.shape, f32),
            pltpu.VMEM((PEERS, *meta.shape), f32),
            pltpu.VMEM((PEERS, capacity, d_model), bf16),
            pltpu.VMEM((PEERS, 8, tok_dev), f32),
            pltpu.VMEM((2, 2, tok_dev, d_model), bf16),
            pltpu.VMEM((chunks, 3, NZ, NY, block, CHUNK), bf16),
            pltpu.VMEM((chunks, 3, NZ, NY, block, CHUNK), f32),
            pltpu.VMEM((SETS, 2, 3, NY // 2, block, half), f32),
            pltpu.VMEM((SETS, 2, 3, 3, NY, block, half), f32),
            pltpu.VMEM((SETS, 2, 3, 16, half), f32),
            pltpu.VMEM((SETS, 2, 3, block, half), f32),
            pltpu.VMEM((SETS, 2, 3, NZ // 2, block, half), f32),
            pltpu.VMEM((SETS, 2, 3, NZ, block, half), f32),
            pltpu.VMEM((SETS, 2, 3, 16, half), f32),
            pltpu.VMEM((SETS, 2, 3, 3, block, half), f32),
            pltpu.VMEM((n_rows, d_model), bf16),
            pltpu.VMEM((n_rows, d_model), bf16),
            pltpu.VMEM((n_rows, d_model), bf16),
            pltpu.VMEM((d_model, n_rows), bf16),
            pltpu.VMEM((d_model, n_rows), bf16),
            pltpu.VMEM((3, n_rows, CHUNK), bf16),
            pltpu.VMEM((n_rows, d_model), f32),
            pltpu.VMEM((n_rows, 128), f32),
            pltpu.VMEM((PEERS, 8, tok_dev), f32),
            dma((2, 2)), dma((2,)), dma((21,)), dma((21,)),
            dma((chunks, 2, 2)), dma((chunks, HOPS, 2, 2)),
            dma((PEERS - 1, 2)), dma((PEERS - 1, 2)),
            dma((chunks, 2, 2)), dma((chunks, HOPS, 2, 2)),
            pltpu.SemaphoreType.REGULAR((chunks - SETS,)),
        ],
        compiler_params=pltpu.CompilerParams(
            collective_id=0, has_side_effects=True, vmem_limit_bytes=67043328),
        name="moe_step",
    )(x_tok, dy_tok, ids, route, w1, w3, w2t)


def solution(mesh):
    tok_spec = P(("fsdp", "ep"), None)
    spec_in = P("ep", "fsdp", None)
    spec_out = P("ep", None, "fsdp")

    def per_device(x_tok, dy_tok, expert_ids, route_w, w_gate, w_up, w_down):
        tok_dev, top_k = expert_ids.shape
        capacity = capacity_of(tok_dev, top_k, PEERS)
        gx, rw, g1, g3, g2, _, _ = moe_step(
            x_tok, dy_tok, expert_ids.T, route_w.T, w_gate[0], w_up[0], w_down[0].T, capacity)
        return gx, rw.T, g1[None], g3[None], g2.T[None]

    return jax.shard_map(
        per_device, mesh=mesh,
        in_specs=(tok_spec, tok_spec, tok_spec, tok_spec, spec_in, spec_in, spec_out),
        out_specs=(tok_spec, tok_spec, spec_in, spec_in, spec_out),
        check_vma=False)
```

time: 945 us -> 216 us (0.23)
  waiting for transfers between devices: 716 us -> 0 us
  Pallas kernels: 0 us -> 207 us
  matrix products: 97.6 us -> 0 us
  local copies, waits for them, and re-layouts: 48 us -> 7.87 us
  blocking collectives: 33.3 us -> 0 us
  starting transfers between devices: 20.5 us -> 0 us
  between operations: 15 us -> 0.64 us
  other arithmetic: 14 us -> 0 us
    reduce_scatter x2 -> x0, waiting for transfers between devices: 456 us -> none  [the longest x1 229 us: per_device(): lax.psum_scatter(dw_gate, 'fsdp', scatter_dimension=1, tiled=True)]
    pallas_call x0 -> x1, Pallas kernels: none -> 207 us  [moe_step(): pl.pallas_call(moe_kernel, out_shape=(jax.ShapeDtypeStruct((tok_dev, d_mo...]
    all_gather x3 -> x0, waiting for transfers between devices: 134 us -> none  [the longest x1 68.7 us: per_device(): w_up_full = lax.all_gather(w_up, 'fsdp', axis=1, tiled=True)]
    dot_general x9 -> x0, matrix products: 97.6 us -> none  [the longest x1 21.3 us: expert_backward(): jnp.einsum('secd,edf->secf', x_rows, w_up_full, preferred_element_type=jn...]
    unnamed x7 -> x0, waiting for transfers between devices: 91.9 us -> none
    all_to_all x1 -> x0, blocking collectives: 33.3 us -> none  [per_device(): lax.all_to_all(x_send, 'ep', 0, 0, tiled=True)]
    all_to_all x4 -> x0, waiting for transfers between devices: 33.2 us -> none  [the longest x1 22.4 us: per_device(): lax.all_to_all(dx_rows.reshape(n_ep * exp_local * capacity, d_model), 'ep...]
    gather x8 -> x0, local copies, waits for them, and re-layouts: 25.8 us -> none  [take_rows(): return jnp.take(rows, row_ids, axis=0, mode='fill', fill_value=0)]
  transfers between devices with their start and end apart: 10 -> 0, of which waited for: 8 -> 0; matrix products, arithmetic and copies ran while one was open for 12% -> 0% of each run, Pallas kernels for 0% -> 0%
where the time goes in v1:
time: 216 us
  Pallas kernels  207 us (96%)
  local copies, waits for them, and re-layouts  7.87 us (4%)
    pallas_call x1, Pallas kernels, moe_step(): pl.pallas_call(moe_kernel, out_shape=(jax.ShapeDtypeStruct((tok_dev, d_mo...  207 us
    unnamed x5, local copies, waits for them, and re-layouts  7.87 us

profile of v1, /device:TPU:2, one launch (start us, length us, event | category | flops | bytes accessed | tf_op | source)
XLA Modules:
  0.0 215.8 jit_solution(9205090984763652389)
XLA Ops:
  0.6 207.3 %moe_step.1 = (bf16[256,768]{1,0:T(8,128)(2,1)}, f32[2,256]{1,0:T(2,128)}, f32[24,2048]{1,0:T(8,128)}, f32[24,2048]{1,0:T(8,128)}, f32[24,2048]{1,0:T(8,128)}, /...) custom-call(bf16[256,768]{1,0:T(8,128)(2,1)} %x_hbm.1, bf16[256,768]{1,0:T(8,128)(2,1)} %dy_hbm.1, ...), custom_call_target="tpu_custom_call" | custom-call | tf_op jit(solution)/shard_map/moe_step/pallas_call | solution.py:407
  207.9 1.8 copy.17
  209.7 1.3 copy.18
  210.9 1.6 copy.19
  212.6 1.6 copy.20
  214.2 1.6 copy.21

commit v2 on v1

--- a/solution.py
+++ b/solution.py
@@ -35,7 +35,7 @@
     return lax.dot_general(a, b, (((ca,), (cb,)), ((), ())), preferred_element_type=jnp.float32)
 
 
-def moe_kernel(x_hbm, dy_hbm, ids_ref, r_ref, w1_ref, w3_ref, w2_ref, gx_out, rw_out, g1_out, g3_out, g2_out, x_all, dy_all,
+def moe_kernel(x_hbm, dy_hbm, ids_ref, r_ref, w1_ref, w3_ref, w2_ref, gx_out, rw_out, g_out, x_all, dy_all,
                meta_ref, meta_all, dx_in, dr_in, tok, wbuf, dw, az_half, az, ay_part, ay, by_half, by, bz_part, bz,
                xs, dys, gs, xt, gt, hid, dx_acc, dr_acc, dr_send,
                tok_sem, loc_sem, tsend, trecv, wsend, wrecv, xsend, xrecv, gsend, grecv, free_sem):
@@ -102,23 +102,28 @@
             device_id={"fsdp": to}, device_id_type=MESH)
 
     def gather_round(a):
+        @pl.when(a < chunks)
+        def _():
+            for v in (0, 1):
+                for d in (0, 1):
+                    wcopy(lax.min(a, chunks - 1), 0, v, d).start()
+
         def one(c, carry):
-            for h in range(HOPS + 1):
+            for h in range(1, HOPS + 1):
                 @pl.when(a - c == h)
                 def _(h=h):
                     for v in (0, 1):
                         together = h == (2, 4)[v]
                         for d in (0, 1):
-                            if h:
-                                wcopy(c, h - 1, v, d).wait_recv()
-                                wcopy(c, h - 1, v, d).wait_send()
+                            wcopy(c, h - 1, v, d).wait_recv()
+                            wcopy(c, h - 1, v, d).wait_send()
                             if h < HOPS and not together:
                                 wcopy(c, h, v, d).start()
                         if together:
                             for d in (0, 1):
                                 wcopy(c, h, v, d).start()
             return carry
-        lax.fori_loop(lax.max(a - HOPS, 0), lax.min(a + 1, chunks), one, 0)
+        lax.fori_loop(lax.max(a - HOPS, 0), lax.min(a, chunks), one, 0)
 
     def tcopy(n, which, block, to, own_block=False):
         src, dst = ((x_hbm, x_all), (dy_hbm, dy_all), (meta_ref, meta_all))[which]
@@ -218,15 +223,24 @@
         lo = lax.max(lax.div(q - HOPS + rounds - 1 + rounds * chunks, rounds) - chunks - 1, 0)
         hi = lax.min(lax.div(q, rounds), chunks)
 
+        new = lax.div(q, rounds) - 1
+
+        @pl.when(jnp.logical_and(lax.rem(q, rounds) == 0, jnp.logical_and(new >= 0, new < chunks)))
+        def _():
+            c = lax.min(lax.max(new, 0), chunks - 1)
+
+            @pl.when(c >= SETS)
+            def _():
+                pl.semaphore_wait(free_sem.at[lax.max(c - SETS, 0)], 4)
+            for v in (0, 1):
+                for d in (0, 1):
+                    gcopy(c, 0, v, d).start()
+
         def one(c, carry):
             s = q - (c + 1) * rounds
-            for h in range(HOPS + 1):
+            for h in range(1, HOPS + 1):
                 @pl.when(s == h)
                 def _(h=h):
-                    if h == 0:
-                        @pl.when(c >= SETS)
-                        def _():
-                            pl.semaphore_wait(free_sem.at[lax.max(c - SETS, 0)], 4)
                     for v in (0, 1):
                         together = h - 1 in last_of_phase[v]
                         if together:
@@ -239,8 +253,7 @@
                                 gcopy(c, h, v, d).start()
                     if h == HOPS:
                         out = pl.ds(pl.multiple_of(c * CHUNK, CHUNK), CHUNK)
-                        for n, g in enumerate((g1_out, g3_out, g2_out)):
-                            g[:, out] = dw[c, n, z, y]
+                        g_out[:, :, out] = dw[c, :, z, y]
 
                         @pl.when(c + SETS < chunks)
                         def _():
@@ -369,15 +382,15 @@
     def step(t, carry):
         n = t - lead
         c, r = lax.div(lax.max(n, 0), rounds), lax.rem(lax.max(n, 0), rounds)
+        @pl.when(r == 0)
+        def _():
+            gather_round(lax.min(t, lead) + c)
         for j in range(rounds):
             @pl.when(jnp.logical_and(jnp.logical_and(n >= 0, t < steps), r == j))
             def _(j=j):
                 for u in range(0 if j == 0 else SERVE[j - 1] + 1, SERVE[j] + 1):
                     compute(c, u)
 
-        @pl.when(r == 0)
-        def _():
-            gather_round(lax.min(t, lead) + c)
         for at, event in ((1, tokens_1), (3, tokens_3), (4, tokens_4), (5, tokens_5), (6, tokens_6),
                           (steps, send_back), (steps + HOPS - 1, combine)):
             pl.when(t == at)(event)
@@ -402,14 +415,14 @@
     hbm = pl.BlockSpec(memory_space=pl.ANY)
     dma = pltpu.SemaphoreType.DMA
     landing = jax.ShapeDtypeStruct((PEERS, tok_dev, d_model), bf16)
-    grad = jax.ShapeDtypeStruct((block, width), f32)
+    grad = jax.ShapeDtypeStruct((3, block, width), f32)
     meta = jax.ShapeDtypeStruct((2 * PEERS, tok_dev), f32)
     return pl.pallas_call(
         moe_kernel,
         out_shape=(jax.ShapeDtypeStruct((tok_dev, d_model), bf16), jax.ShapeDtypeStruct(route.shape, f32),
-                   grad, grad, grad, landing, landing),
+                   grad, landing, landing),
         in_specs=[hbm, hbm] + [vmem] * 5,
-        out_specs=[vmem] * 5 + [hbm, hbm],
+        out_specs=[vmem] * 3 + [hbm, hbm],
         scratch_shapes=[
             pltpu.VMEM(meta.shape, f32),
             pltpu.VMEM((PEERS, *meta.shape), f32),
@@ -455,9 +468,9 @@
     def per_device(x_tok, dy_tok, expert_ids, route_w, w_gate, w_up, w_down):
         tok_dev, top_k = expert_ids.shape
         capacity = capacity_of(tok_dev, top_k, PEERS)
-        gx, rw, g1, g3, g2, _, _ = moe_step(
+        gx, rw, g, _, _ = moe_step(
             x_tok, dy_tok, expert_ids.T, route_w.T, w_gate[0], w_up[0], w_down[0].T, capacity)
-        return gx, rw.T, g1[None], g3[None], g2.T[None]
+        return gx, rw.T, g[0][None], g[1][None], g[2].T[None]
 
     return jax.shard_map(
         per_device, mesh=mesh,

time: 216 us -> 213 us (0.986)
  local copies, waits for them, and re-layouts: 7.87 us -> 4.93 us
    unnamed x5 -> x2, local copies, waits for them, and re-layouts: 7.87 us -> 3 us
where the time goes in v2:
time: 213 us
  Pallas kernels  207 us (97%)
  local copies, waits for them, and re-layouts  4.93 us (2%)
    pallas_call x1, Pallas kernels, moe_step(): pl.pallas_call(moe_kernel, out_shape=(jax.ShapeDtypeStruct((tok_dev, d_mo...  207 us

profile of v2, /device:TPU:2, one launch (start us, length us, event | category | flops | bytes accessed | tf_op | source)
XLA Modules:
  0.0 212.7 jit_solution(1774429309756417632)
XLA Ops:
  0.6 207.1 %moe_step.1 = (bf16[256,768]{1,0:T(8,128)(2,1)}, f32[2,256]{1,0:T(2,128)}, f32[3,24,2048]{2,1,0:T(8,128)}, bf16[8,256,768]{2,1,0:T(8,128)(2,1)}, bf16[8,256,768]{2,1,0:T(8,128)(2,1)}) custom-call(bf16[256,768]{1,0:T(8,128)(2,1)} %x_hbm.1, bf16[256,768]{1,0:T(8,128)(2,1)} %dy_hbm.1, s32[2,256]{1,0:T(2,128)} %bitcast.17, f32[2,256]{1,0:T(2,128)} %bitcast.18, ...), custom_call_target="tpu_custom_call" | custom-call | tf_op jit(solution)/shard_map/moe_step/pallas_call | solution.py:420
  207.7 1.9 slice_bitcast_fusion
  209.7 1.8 copy.14
  211.4 1.2 copy.15
